TPU v7x, 256 devices: a whole 4x4x8 slice. The times are simulated.
256 devices in a mesh: pair: 64 (over x, z, y_hi), col: 2 (over y_lo), freq: 2 (over core).
Axes of the slice: x: 4, y: 4 (y_hi: 2, y_lo: 2; y = y_hi * 2 + y_lo), z: 8, core: 2. Of those that a mesh axis runs over, the one named last changes fastest.
Arguments:
- pair_matrix: bfloat16 [196608, 2048], P('pair', 'col'), may hold values from -0.0390625 to 0.0390625
- energies: float32 [196608], P('pair'), may hold values from 0.5 to 20
- omega: float32 [2], P('freq'), may hold values from 0.2 to 10
Outputs:
- chi: float32 [2048, 2, 2048], P('pair', 'freq', 'col')
All inputs are finite; a program needn't handle non-finite values.
Results may differ from a plain program's by a relative error of at most 0.00053.
Values may be sent and summed in bfloat16 or wider, within the bound.
A program may use at most 128 MiB of HBM per device.

v0:
```python
import jax
import jax.numpy as jnp
from jax import lax
from jax.sharding import Mesh
from jax.sharding import PartitionSpec as P

PAIR = ("pair_0", "pair_1", "pair_2")


def summed_rows(subtotal, axes):
    for axis in axes:
        subtotal = lax.psum_scatter(subtotal, axis, scatter_dimension=0, tiled=True)
    return subtotal


def cut_along(value, dim, peers):
    dims = value.shape
    pieces = value.reshape(*dims[:dim], peers, dims[dim] // peers, *dims[dim + 1 :])
    return jnp.moveaxis(pieces, dim, 0)


def sum_at_owner(value, axis, dim):
    peers = lax.axis_size(axis)
    pieces = lax.all_to_all(cut_along(value, dim, peers), axis, 0, 0, tiled=True)
    return jnp.sum(pieces, axis=0)


def negative_gram(left, right):
    return -lax.dot_general(
        left, right, (((0,), (0,)), ((), ())), preferred_element_type=jnp.float32
    )


def per_device(pair_matrix, energies, omega):
    freq_value = omega[0]
    factor = jnp.sqrt(4.0 * energies / (energies * energies + freq_value * freq_value))
    scaled = (factor[:, None] * pair_matrix.astype(jnp.float32)).astype(jnp.bfloat16)
    halves = lax.all_to_all(scaled, "col", split_axis=0, concat_axis=1, tiled=True)
    rows_whole = summed_rows(negative_gram(halves, halves), PAIR)
    owned = sum_at_owner(rows_whole, "col", 1)
    return owned[:, None, :]


def solution(mesh):
    finer = Mesh(
        mesh.devices.reshape(4, 8, 2, mesh.shape["col"], mesh.shape["freq"]),
        ("pair_0", "pair_1", "pair_2", "col", "freq"),
    )
    in_specs = (P(PAIR, "col"), P(PAIR), P("freq"))
    out_specs = P(PAIR, "freq", "col")
    return jax.shard_map(
        per_device, mesh=finer, in_specs=in_specs, out_specs=out_specs, check_vma=False
    )
```

profile of v0, /device:TPU:6, one launch (start us, length us, event | category | flops | bytes accessed | tf_op | source)
XLA Modules:
  0.0 364.0 jit_solution(6178675632255771245)
XLA Ops:
  6.5 0.0 reduce-scatter.4.cloned.1.call-start
  7.2 0.7 divide_sqrt_fusion
  7.9 3.9 %multiply_convert_fusion = bf16[3072,1024]{1,0:T(8,128)(2,1)S(1)} fusion(bf16[3072,1024]{1,0:T(8,128)(2,1)} %param.3, f32[3072]{0:T(1024)S(1)} %divide_sqrt_fusion), kind=kLoop, calls=%fused_computation | loop fusion | flops 9437184 | bytes 12595200 | tf_op jit(solution)/shard_map/convert_element_type | solution.py:37
  11.8 74.1 %all_to_all.24 = bf16[2,1536,1024]{2,1,0:T(8,128)(2,1)} all-to-all(bf16[2,1536,1024]{2,1,0:T(8,128)(2,1)S(1)} %bitcast.13), channel_id=1, replica_groups=mesh['pair_0'=4,'pair_1'=8,'pair_2'=2,'col'=2,'freq'=2] {'col'}, dimensions={0} | all-to-all | bytes 12582912 | tf_op jit(solution)/shard_map/all_to_all | solution.py:38
  85.9 8.7 %copy.5 = bf16[1536,2,1024]{0,2,1:T(8,128)(2,1)} copy(bf16[1536,2,1024]{2,0,1:T(8,128)(2,1)} %bitcast.14) | data formatting | bytes 12582912 | tf_op jit(solution)/shard_map/all_to_all | solution.py:38
  94.6 19.8 %convolution_negate_fusion = f32[2048,2048]{1,0:T(8,128)} fusion(bf16[1536,2048]{0,1:T(8,128)(2,1)} %bitcast.15), kind=kOutput, calls=%fused_computation.1 | convolution fusion | flops 12889096192 | bytes 23068672 | tf_op jit(solution)/shard_map/dot_general | solution.py:29
  114.4 0.0 reduce-scatter.4.cloned.1.call-update
  114.5 0.0 reduce-scatter.6.cloned.1.call-start
  114.5 151.6 %reduce-scatter.4.cloned.1.call-done = f32[512,2048]{1,0:T(8,128)} async-done(((f32[2048,2048]{1,0:T(8,128)}), f32[512,2048]{1,0:T(8,128)}) %reduce-scatter.4.cloned.1.call-update) | async-done | bytes 4194320 | tf_op jit(solution)/shard_map/reduce_scatter | solution.py:12
  266.2 0.0 reduce-scatter.6.cloned.1.call-update
  266.2 0.0 reduce-scatter.8.cloned.1.call-start
  266.2 59.4 %reduce-scatter.6.cloned.1.call-done = f32[64,2048]{1,0:T(8,128)} async-done(((f32[512,2048]{1,0:T(8,128)}), f32[64,2048]{1,0:T(8,128)}) %reduce-scatter.6.cloned.1.call-update) | async-done | bytes 524304 | tf_op jit(solution)/shard_map/reduce_scatter | solution.py:12
  325.7 0.0 reduce-scatter.8.cloned.1.call-update
  325.7 22.4 %reduce-scatter.8.cloned.1.call-done = f32[32,2048]{1,0:T(8,128)} async-done(((f32[64,2048]{1,0:T(8,128)}), f32[32,2048]{1,0:T(8,128)}) %reduce-scatter.8.cloned.1.call-update) | async-done | bytes 262160 | tf_op jit(solution)/shard_map/reduce_scatter | solution.py:12
  348.1 1.0 copy.9
  349.1 7.7 %all_to_all.25 = f32[2,32,1024]{2,1,0:T(8,128)S(1)} all-to-all(f32[2,32,1024]{2,1,0:T(8,128)S(1)} %bitcast.16), channel_id=1, replica_groups=mesh['pair_0'=4,'pair_1'=8,'pair_2'=2,'col'=2,'freq'=2] {'col'}, dimensions={0} | all-to-all | bytes 524288 | tf_op jit(solution)/shard_map/all_to_all | solution.py:24
  356.8 0.7 broadcast_in_dim.4
  (1 shorter events, 0.0 us)
Async XLA Ops:
  6.5 259.6 %reduce-scatter.4.cloned.1.call-start = ((), (), s32[]{:S(2)}) async-start(), calls=%async_computation.5 | async-start | bytes 20971520 | tf_op jit(solution)/shard_map/reduce_scatter | solution.py:12
  114.5 211.2 %reduce-scatter.6.cloned.1.call-start = ((), (), s32[]{:S(2)}) async-start(), calls=%async_computation.6 | async-start | bytes 4718592 | tf_op jit(solution)/shard_map/reduce_scatter | solution.py:12
  266.2 81.9 %reduce-scatter.8.cloned.1.call-start = ((), (), s32[]{:S(2)}) async-start(), calls=%async_computation.7 | async-start | bytes 786432 | tf_op jit(solution)/shard_map/reduce_scatter | solution.py:12
Sparse Core Ops, SparseCore 0:
  114.6 151.5 reduce-scatter.3
  268.7 56.9 reduce-scatter.5
  328.2 19.8 reduce-scatter.7
where the time goes:
time: 365 us; the launch traced here: 364 us
  waiting for transfers between devices  234 us (64%)
  blocking collectives  81.8 us (22%)
  matrix products  19.8 us (5%)
  between operations  13.8 us (4%)
  local copies, waits for them, and re-layouts  10.4 us (3%)
  other arithmetic  4.6 us (1%)
    reduce_scatter x3, waiting for transfers between devices, summed_rows(): subtotal = lax.psum_scatter(subtotal, axis, scatter_dimension=0, tiled=True)  233 us
    all_to_all x1, blocking collectives, per_device(): lax.all_to_all(scaled, 'col', split_axis=0, concat_axis=1, tiled=True)  74.1 us
    dot_general x1, matrix products, negative_gram(): lax.dot_general(left, right, (((0,), (0,)), ((), ())), preferred_element_...  19.8 us
    all_to_all x1, local copies, waits for them, and re-layouts, per_device(): lax.all_to_all(scaled, 'col', split_axis=0, concat_axis=1, tiled=True)  8.67 us
    all_to_all x1, blocking collectives, sum_at_owner(): lax.all_to_all(cut_along(value, dim, peers), axis, 0, 0, tiled=True)  7.67 us
  transfers between devices with their start and end apart: 3, of which 3 were waited for; matrix products, arithmetic and copies ran while one was open for 0% of the time, Pallas kernels for 0%

commit v1 on v0

v1 whole, which is shorter than its diff:
```python
import jax
import jax.numpy as jnp
from jax import lax
from jax.experimental import pallas as pl
from jax.experimental.pallas import tpu as pltpu
from jax.sharding import Mesh
from jax.sharding import PartitionSpec as P

MESH = pl.DeviceIdType.MESH
ROWS = ("x", "z", "h")
ORDER = (0, 2, 1, 3)


def gram(left, right):
    return -lax.dot_general(
        left, right, (((0,), (0,)), ((), ())), preferred_element_type=jnp.float32
    )


def kernel(
    e_ref,
    w_ref,
    x_hbm,
    out_ref,
    own,
    fac,
    raw,
    other,
    part,
    relay,
    from_left,
    from_right,
    load_sem,
    y_send,
    y_recv,
    d_send,
    d_recv,
    x_send,
    relay_recv,
    left_recv,
    right_recv,
):
    x = lax.axis_index("x")
    low = lax.axis_index("l")
    core = lax.axis_index("f")
    right = lax.rem(x + 1, 4)
    left = lax.rem(x + 3, 4)
    pairs, cols = own.shape
    half = pairs // 2
    quarter = half // 2
    width = cols // 4
    mid = width // 2

    barrier = pltpu.get_barrier_semaphore()
    for peer in ({"x": right}, {"x": left}, {"l": 1 - low}, {"f": 1 - core}):
        pl.semaphore_signal(barrier, inc=1, device_id=peer, device_id_type=MESH)
    pl.semaphore_wait(barrier, 4)

    mine = pl.ds(pl.multiple_of(core * quarter, quarter), quarter)
    theirs = pl.ds(pl.multiple_of((1 - core) * quarter, quarter), quarter)
    leaving = pl.ds(pl.multiple_of((1 - low) * half + core * quarter, quarter), quarter)

    def y_copy(j):
        return pltpu.make_async_remote_copy(
            src_ref=x_hbm.at[leaving, pl.ds(j * width, width)],
            dst_ref=raw.at[j, mine],
            send_sem=y_send.at[j],
            recv_sem=y_recv.at[j],
            device_id={"l": 1 - low},
            device_id_type=MESH,
        )

    def d_copy(j, rows):
        return pltpu.make_async_remote_copy(
            src_ref=raw.at[j, rows],
            dst_ref=raw.at[j, rows],
            send_sem=d_send.at[j],
            recv_sem=d_recv.at[j],
            device_id={"f": 1 - core},
            device_id_type=MESH,
        )

    for j in ORDER:
        y_copy(j).start()
    loads = load_sem.shape[0]
    block = pairs // loads
    for b in range(loads):
        pltpu.make_async_copy(
            x_hbm.at[pl.ds(b * block, block)], own.at[pl.ds(b * block, block)], load_sem.at[b]
        ).start()

    freq = w_ref[0]

    @pl.loop(0, pairs // 128)
    def _(b):
        energy = e_ref[pl.ds(b, 1), :]
        value = jnp.sqrt(4.0 * energy / (energy * energy + freq * freq))
        fac[pl.ds(pl.multiple_of(b * 128, 128), 128), :] = jnp.broadcast_to(value, (128, 128)).T

    for b in range(loads):
        pltpu.make_async_copy(
            x_hbm.at[pl.ds(b * block, block)], own.at[pl.ds(b * block, block)], load_sem.at[b]
        ).wait()

        @pl.loop(0, block // 64)
        def _(i):
            rows = pl.ds(pl.multiple_of(b * block + i * 64, 64), 64)
            scale = fac[rows, :]
            for c in range(cols // 128):
                lanes = pl.ds(c * 128, 128)
                own[rows, lanes] = (scale * own[rows, lanes].astype(jnp.float32)).astype(jnp.bfloat16)

    def distance(k):
        dest = (2 * low if k < 4 else 2 * (1 - low)) + (k % 4) // 2
        return lax.rem(dest - x + 4, 4)

    def x_copy(k, side, to_right, relayed):
        rows = pl.ds(side * mid, mid)
        inbox = from_left if to_right else from_right
        inbox_sem = left_recv if to_right else right_recv
        return pltpu.make_async_remote_copy(
            src_ref=part.at[k, rows],
            dst_ref=relay.at[k] if relayed else inbox.at[k % 2, rows],
            send_sem=x_send.at[k, side],
            recv_sem=relay_recv.at[k] if relayed else inbox_sem.at[k % 2, side],
            device_id={"x": right if to_right else left},
            device_id_type=MESH,
        )

    def send_direct(k):
        far = distance(k)

        @pl.when(far == 2)
        def _():
            x_copy(k, 0, True, True).start()
            x_copy(k, 1, False, True).start()

        @pl.when(far == 1)
        def _():
            x_copy(k, 1, True, False).start()

        @pl.when(far == 3)
        def _():
            x_copy(k, 0, False, False).start()

    def send_relayed(k):
        far = distance(k)
        for away, side, to_right in ((1, 0, True), (3, 1, False)):

            @pl.when(far == away)
            def _():
                x_copy(k, side, to_right, True).wait_recv()

                @pl.loop(0, mid // 8)
                def _(i):
                    at = pl.multiple_of(i * 8, 8)
                    rows = pl.ds(side * mid + at, 8)
                    part[k, rows, :] = part[k, rows, :] + relay[k, pl.ds(at, 8), :]

                x_copy(k, side, to_right, False).start()

    def finish(k):
        @pl.when(distance(k) == 0)
        def _():
            for side in range(2):
                x_copy(k, side, True, False).wait_recv()
                x_copy(k, side, False, False).wait_recv()
            i = k % 2

            @pl.loop(0, width // 8)
            def _(r):
                at = pl.ds(pl.multiple_of(r * 8, 8), 8)
                out_ref[pl.ds(pl.multiple_of(i * width + r * 8, 8), 8), :] = (
                    part[k, at, :] + from_left[i, at, :] + from_right[i, at, :]
                )

        @pl.when(distance(k) != 0)
        def _():
            for side in range(2):
                x_copy(k, side, True, False).wait_send()

    for k in ORDER:
        part[k] = gram(own[:, k * width : (k + 1) * width], own[...])
        send_direct(k)

    pending = list(ORDER)
    mine_half = pl.ds(pl.multiple_of(low * half, half), half)
    for j in ORDER:
        y_copy(j).wait_recv()
        d_copy(j, mine).start()
        d_copy(j, theirs).wait_recv()

        @pl.loop(0, half // 64)
        def _(i):
            at = pl.multiple_of(i * 64, 64)
            scale = fac[pl.ds(pl.multiple_of(low * half + i * 64, 64), 64), :]
            for c in range(width // 128):
                lanes = pl.ds(c * 128, 128)
                other[pl.ds(at, 64), lanes] = (
                    scale * raw[j, pl.ds(at, 64), lanes].astype(jnp.float32)
                ).astype(jnp.bfloat16)

        part[4 + j] = gram(other[...], own[mine_half, :])
        send_direct(4 + j)
        send_relayed(pending.pop(0))
        pending.append(4 + j)
    for k in pending:
        send_relayed(k)
    for k in range(8):
        finish(k)
    for j in range(4):
        y_copy(j).wait_send()
        d_copy(j, mine).wait_send()


def column_sums(pair_matrix, energies, omega):
    pairs, cols = pair_matrix.shape
    width = cols // 4
    vmem, dma = pltpu.VMEM, pltpu.SemaphoreType.DMA
    loads = 6
    return pl.pallas_call(
        kernel,
        out_shape=jax.ShapeDtypeStruct((2 * width, cols), jnp.float32),
        in_specs=[
            pl.BlockSpec(memory_space=pltpu.VMEM),
            pl.BlockSpec(memory_space=pltpu.SMEM),
            pl.BlockSpec(memory_space=pl.ANY),
        ],
        out_specs=pl.BlockSpec(memory_space=pltpu.VMEM),
        scratch_shapes=[
            vmem((pairs, cols), jnp.bfloat16),
            vmem((pairs, 128), jnp.float32),
            vmem((4, pairs // 2, width), jnp.bfloat16),
            vmem((pairs // 2, width), jnp.bfloat16),
            vmem((8, width, cols), jnp.float32),
            vmem((8, width // 2, cols), jnp.float32),
            vmem((2, width, cols), jnp.float32),
            vmem((2, width, cols), jnp.float32),
            dma((loads,)),
            dma((4,)),
            dma((4,)),
            dma((4,)),
            dma((4,)),
            dma((8, 2)),
            dma((8,)),
            dma((2, 2)),
            dma((2, 2)),
        ],
        compiler_params=pltpu.CompilerParams(
            collective_id=0, has_side_effects=True, vmem_limit_bytes=60 * 1024 * 1024
        ),
    )(energies.reshape(pairs // 128, 128), omega, pair_matrix)


def per_device(pair_matrix, energies, omega):
    summed = column_sums(pair_matrix, energies, omega)
    summed = lax.psum_scatter(summed, "z", scatter_dimension=0, tiled=True)
    owned = lax.psum_scatter(summed, "h", scatter_dimension=0, tiled=True)
    rows, cols = owned.shape
    pieces = jnp.moveaxis(owned.reshape(rows, 2, 16, rows), 2, 0)
    pieces = lax.all_to_all(pieces, ("z", "h"), 0, 0, tiled=True)
    pieces = jnp.transpose(pieces, (2, 3, 0, 1)).reshape(2, rows, 16 * rows)
    x, low = lax.axis_index("x"), lax.axis_index("l")
    bit = lax.rem(x, 2)
    got = []
    for k in range(2):
        perm = [
            ((2 * (1 - m) + b) * 2 + m, (2 * m + (b ^ k)) * 2 + 1 - m) for m in range(2) for b in range(2)
        ]
        sent = jnp.where((bit + k) % 2 == 0, pieces[0], pieces[1])
        got.append(lax.ppermute(sent, ("x", "l"), perm))
    first = jnp.where(bit == 0, got[0], got[1])
    second = jnp.where(bit == 0, got[1], got[0])
    owned = owned + jnp.concatenate([first, second], axis=1)
    return owned[:, None, :]


def solution(mesh):
    finer = Mesh(mesh.devices.reshape(4, 8, 2, 2, 2), ("x", "z", "h", "l", "f"))
    return jax.shard_map(
        per_device,
        mesh=finer,
        in_specs=(P(ROWS, "l"), P(ROWS), P("f")),
        out_specs=P(ROWS, "f", "l"),
        check_vma=False,
    )
```

time: 365 us -> 208 us (0.57)
  waiting for transfers between devices: 234 us -> 80.9 us
  Pallas kernels: 0 us -> 91 us
  blocking collectives: 81.8 us -> 0 us
  matrix products: 19.8 us -> 0 us
  starting transfers between devices: 0.08 us -> 15.4 us
  local copies, waits for them, and re-layouts: 10.4 us -> 4.53 us
    reduce_scatter x3 -> x2, waiting for transfers between devices: 233 us -> 65.5 us  [the longest x1 46.2 us: per_device(): summed = lax.psum_scatter(summed, 'z', scatter_dimension=0, tiled=True)]
    pallas_call x0 -> x1, Pallas kernels: none -> 91 us  [column_sums(): pl.pallas_call(kernel, out_shape=jax.ShapeDtypeStruct((2 * width, cols),...]
    all_to_all x2 -> x0, blocking collectives: 81.8 us -> none  [the longest x1 74.1 us: per_device(): lax.all_to_all(scaled, 'col', split_axis=0, concat_axis=1, tiled=True)]
    dot_general x1 -> x0, matrix products: 19.8 us -> none  [negative_gram(): lax.dot_general(left, right, (((0,), (0,)), ((), ())), preferred_element_...]
    all_to_all x0 -> x1, waiting for transfers between devices: none -> 11.1 us  [per_device(): pieces = lax.all_to_all(pieces, ('z', 'h'), 0, 0, tiled=True)]
    ppermute x0 -> x2, starting transfers between devices: none -> 8.23 us  [per_device(): got.append(lax.ppermute(sent, ('x', 'l'), perm))]
    all_to_all x1, local copies, waits for them, and re-layouts: 8.67 us -> 0.51 us  [per_device(): pieces = lax.all_to_all(pieces, ('z', 'h'), 0, 0, tiled=True)]
    all_to_all x0 -> x1, starting transfers between devices: none -> 7.1 us  [per_device(): pieces = lax.all_to_all(pieces, ('z', 'h'), 0, 0, tiled=True)]
  transfers between devices with their start and end apart: 3 -> 5, of which waited for: 3 -> 4; matrix products, arithmetic and copies ran while one was open for 0% -> 0% of each run, Pallas kernels for 0% -> 0%
where the time goes in v1:
time: 208 us; the launch traced here: 207 us
  Pallas kernels  91 us (44%)
  waiting for transfers between devices  80.9 us (39%)
  starting transfers between devices  15.4 us (7%)
  between operations  14.2 us (7%)
  local copies, waits for them, and re-layouts  4.53 us (2%)
    pallas_call x1, Pallas kernels, column_sums(): pl.pallas_call(kernel, out_shape=jax.ShapeDtypeStruct((2 * width, cols),...  91 us
    reduce_scatter x1, waiting for transfers between devices, per_device(): summed = lax.psum_scatter(summed, 'z', scatter_dimension=0, tiled=True)  46.2 us
    reduce_scatter x1, waiting for transfers between devices, per_device(): owned = lax.psum_scatter(summed, 'h', scatter_dimension=0, tiled=True)  19.3 us
    all_to_all x1, waiting for transfers between devices, per_device(): pieces = lax.all_to_all(pieces, ('z', 'h'), 0, 0, tiled=True)  11.1 us
    ppermute x2, starting transfers between devices, per_device(): got.append(lax.ppermute(sent, ('x', 'l'), perm))  8.23 us
    all_to_all x1, starting transfers between devices, per_device(): pieces = lax.all_to_all(pieces, ('z', 'h'), 0, 0, tiled=True)  7.1 us
    ppermute x2, waiting for transfers between devices, per_device(): got.append(lax.ppermute(sent, ('x', 'l'), perm))  4.24 us
  transfers between devices with their start and end apart: 5, of which 4 were waited for; matrix products, arithmetic and copies ran while one was open for 0% of the time, Pallas kernels for 0%

profile of v1, /device:TPU:6, one launch (start us, length us, event | category | flops | bytes accessed | tf_op | source)
XLA Modules:
  0.0 207.0 jit_solution(1804253786202684599)
XLA Ops:
  6.5 0.0 reduce-scatter.3.cloned.1.call-start
  7.2 91.0 %shard_map.37 = f32[512,1024]{1,0:T(8,128)} custom-call(f32[24,128]{1,0:T(8,128)} %bitcast.15, f32[1]{0:T(128)S(6)} %copy.10.w_ref, bf16[3072,1024]{1,0:T(8,128)(2,1)} %x_hbm.1), custom_call_target="tpu_custom_call" | custom-call | tf_op jit(solution)/shard_map/pallas_call | solution.py:221
  98.2 0.0 reduce-scatter.3.cloned.1.call-update
  98.2 0.0 reduce-scatter.5.cloned.1.call-start
  98.3 46.2 %reduce-scatter.3.cloned.1.call-done = f32[64,1024]{1,0:T(8,128)} async-done(((f32[512,1024]{1,0:T(8,128)}), f32[64,1024]{1,0:T(8,128)}) %reduce-scatter.3.cloned.1.call-update) | async-done | bytes 262160 | tf_op jit(solution)/shard_map/reduce_scatter | solution.py:257
  144.5 0.0 reduce-scatter.5.cloned.1.call-update
  144.5 19.3 %reduce-scatter.5.cloned.1.call-done = f32[32,1024]{1,0:T(8,128)} async-done(((f32[64,1024]{1,0:T(8,128)}), f32[32,1024]{1,0:T(8,128)}) %reduce-scatter.5.cloned.1.call-update) | async-done | bytes 131088 | tf_op jit(solution)/shard_map/reduce_scatter | solution.py:258
  163.8 0.0 copy-start
  163.8 1.1 reshape.16
  165.0 0.3 copy.6
  165.3 0.9 reshape.17
  166.3 7.1 %all-to-all-start = ((f32[16,1,2048]{2,1,0:T(1,128)}), f32[16,1,2048]{2,1,0:T(1,128)S(1)}, u32[]{:S(2)}, u32[]{:S(2)}) async-start(f32[16,1,2048]{2,1,0:T(1,128)} %reshape.17), calls=%async_computation.2 | async-start | bytes 262144 | tf_op jit(solution)/shard_map/all_to_all | solution.py:261
  173.4 11.1 %all-to-all-done = f32[16,1,2048]{2,1,0:T(1,128)S(1)} async-done(((f32[16,1,2048]{2,1,0:T(1,128)}), f32[16,1,2048]{2,1,0:T(1,128)S(1)}, u32[]{:S(2)}, u32[]{:S(2)}) %all-to-all-start) | async-done | bytes 131104 | tf_op jit(solution)/shard_map/all_to_all | solution.py:261
  184.5 0.5 broadcast.7
  185.0 0.9 reduce
  186.0 0.2 reshape.18
  186.2 0.2 copy.7
  186.4 0.1 select_n.45
  186.5 4.2 %collective-permute-start = (f32[32,512]{1,0:T(8,128)S(1)}, f32[32,512]{1,0:T(8,128)S(1)}, u32[]{:S(2)}, u32[]{:S(2)}) collective-permute-start(f32[32,512]{1,0:T(8,128)S(1)} %select_n.45), channel_id=1, source_target_pairs={{128,2},{192,66},{2,128},{66,192},{129,3},{193,67},{3,129},{67,193... | collective-permute-start | bytes 196616 | tf_op jit(solution)/shard_map/ppermute | solution.py:271
  190.8 0.2 copy.8
  190.9 0.1 select_n.49
  191.1 4.0 %collective-permute-start.1 = (f32[32,512]{1,0:T(8,128)S(1)}, f32[32,512]{1,0:T(8,128)S(1)}, u32[]{:S(2)}, u32[]{:S(2)}) collective-permute-start(f32[32,512]{1,0:T(8,128)S(1)} %select_n.49), channel_id=1, source_target_pairs={{128,66},{192,2},{2,192},{66,128},{129,67},{193,3},{3,193},{67,129... | collective-permute-start | bytes 196616 | tf_op jit(solution)/shard_map/ppermute | solution.py:271
  195.1 0.0 collective-permute-done
  195.1 4.2 %collective-permute-done.1 = f32[32,512]{1,0:T(8,128)S(1)} collective-permute-done((f32[32,512]{1,0:T(8,128)S(1)}, f32[32,512]{1,0:T(8,128)S(1)}, u32[]{:S(2)}, u32[]{:S(2)}) %collective-permute-start.1) | collective-permute-done | bytes 65568 | tf_op jit(solution)/shard_map/ppermute | solution.py:271
  199.4 0.0 copy-done
  199.4 0.8 copy.9
  (5 shorter events, 0.2 us)
Async XLA Ops:
  6.5 137.9 %reduce-scatter.3.cloned.1.call-start = ((), (), s32[]{:S(2)}) async-start(), calls=%async_computation.3 | async-start | bytes 2359296 | tf_op jit(solution)/shard_map/reduce_scatter | solution.py:257
  98.2 65.6 %reduce-scatter.5.cloned.1.call-start = ((), (), s32[]{:S(2)}) async-start(), calls=%async_computation.4 | async-start | bytes 393216 | tf_op jit(solution)/shard_map/reduce_scatter | solution.py:258
  163.8 35.5 %copy-start = (f32[32,1024]{1,0:T(8,128)S(1)}, f32[32,1024]{1,0:T(8,128)}, u32[]{:S(2)}) copy-start(f32[32,1024]{1,0:T(8,128)} %reduce-scatter.5.cloned.1.call-done) | copy-start | bytes 393220
  166.3 18.2 %all-to-all-start = ((f32[16,1,2048]{2,1,0:T(1,128)}), f32[16,1,2048]{2,1,0:T(1,128)S(1)}, u32[]{:S(2)}, u32[]{:S(2)}) async-start(f32[16,1,2048]{2,1,0:T(1,128)} %reshape.17), calls=%async_computation.2 | async-start | bytes 262144 | tf_op jit(solution)/shard_map/all_to_all | solution.py:261
  186.5 8.6 %collective-permute-start = (f32[32,512]{1,0:T(8,128)S(1)}, f32[32,512]{1,0:T(8,128)S(1)}, u32[]{:S(2)}, u32[]{:S(2)}) collective-permute-start(f32[32,512]{1,0:T(8,128)S(1)} %select_n.45), channel_id=1, source_target_pairs={{128,2},{192,66},{2,128},{66,192},{129,3},{193,67},{3,129},{67,193... | collective-permute-start | bytes 196616 | tf_op jit(solution)/shard_map/ppermute | solution.py:271
  191.1 8.3 %collective-permute-start.1 = (f32[32,512]{1,0:T(8,128)S(1)}, f32[32,512]{1,0:T(8,128)S(1)}, u32[]{:S(2)}, u32[]{:S(2)}) collective-permute-start(f32[32,512]{1,0:T(8,128)S(1)} %select_n.49), channel_id=1, source_target_pairs={{128,66},{192,2},{2,192},{66,128},{129,67},{193,3},{3,193},{67,129... | collective-permute-start | bytes 196616 | tf_op jit(solution)/shard_map/ppermute | solution.py:271
Sparse Core Ops, SparseCore 0:
  98.4 46.0 reduce-scatter.2
  146.9 16.8 reduce-scatter.4

commit v2 on v0

v2 whole, which is shorter than its diff:
```python
import jax
import jax.numpy as jnp
from jax import lax
from jax.experimental import pallas as pl
from jax.experimental.pallas import tpu as pltpu
from jax.sharding import Mesh
from jax.sharding import PartitionSpec as P

MESH = pl.DeviceIdType.MESH
ROWS = ("x", "z", "h")


def gram(left, right):
    return -lax.dot_general(
        left, right, (((0,), (0,)), ((), ())), preferred_element_type=jnp.float32
    )


def aligned(value, size):
    return pl.ds(pl.multiple_of(value, size), size)


class Ring:
    def __init__(self, axis, n, block, inbox, send_sem, recv_sem):
        self.axis, self.n, self.block, self.inbox = axis, n, block, inbox
        self.send_sem, self.recv_sem = send_sem, recv_sem
        self.pos = lax.axis_index(axis)

    def first(self, way, side):
        return self.n // 2 if way == side else self.n // 2 - 1

    def toward(self, way, dist):
        return lax.rem(self.pos + (dist if way == 0 else self.n - dist), self.n)

    def copy(self, way, side, dist):
        return pltpu.make_async_remote_copy(
            src_ref=self.block(self.toward(way, dist), side),
            dst_ref=self.inbox.at[way, side, dist - 1],
            send_sem=self.send_sem.at[way, side, dist - 1],
            recv_sem=self.recv_sem.at[way, side, dist - 1],
            device_id={self.axis: self.toward(way, 1)},
            device_id_type=MESH,
        )

    def begin(self, way, side):
        self.copy(way, side, self.first(way, side)).start()

    def hop(self, way, side, dist):
        self.copy(way, side, dist + 1).wait_recv()
        held = self.block(self.toward(way, dist), side)
        came = self.inbox.at[way, side, dist]

        @pl.loop(0, held.shape[0] // 16)
        def _(i):
            rows = aligned(i * 16, 16)
            held[rows, :] = held[rows, :] + came[rows, :]

        self.copy(way, side, dist).start()

    def begin_all(self):
        for way, side in ((0, 0), (1, 1), (0, 1), (1, 0)):
            self.begin(way, side)

    def steps(self):
        out = []
        for dist in range(self.n // 2 - 1, 0, -1):
            out.append(((0, 0, dist), (1, 1, dist)))
            if dist > 1:
                out.append(((0, 1, dist - 1), (1, 0, dist - 1)))
        return out

    def arrived(self):
        for way in range(2):
            for side in range(2):
                self.copy(way, side, 1).wait_recv()

    def drain(self):
        for way in range(2):
            for side in range(2):
                for dist in range(self.first(way, side), 0, -1):
                    self.copy(way, side, dist).wait_send()


def kernel(
    e_ref,
    w_ref,
    x_hbm,
    out_ref,
    own,
    fac,
    raw,
    other,
    d_part,
    d_box,
    c_part,
    c_box,
    e_part,
    e_box,
    f_part,
    f_box,
    tile,
    tile_t,
    tile_box,
    d_tile,
    d_tile_box,
    in_d,
    in_n,
    in_t,
    load_sem,
    y_send,
    y_recv,
    s_send,
    s_recv,
    d_send,
    d_recv,
    c_send,
    c_recv,
    e_send,
    e_recv,
    f_send,
    f_recv,
    h_send,
    h_recv,
    in_d_sem,
    in_n_sem,
    in_t_sem,
    out_d_sem,
    out_n_sem,
    out_t_sem,
):
    x, z, h = lax.axis_index("x"), lax.axis_index("z"), lax.axis_index("h")
    low, core = lax.axis_index("l"), lax.axis_index("f")
    pairs, cols = own.shape
    half, width = pairs // 2, cols // 4
    quarter, mid = half // 2, width // 2
    div = lax.div

    barrier = pltpu.get_barrier_semaphore()
    peers = (
        {"x": lax.rem(x + 1, 4)},
        {"x": lax.rem(x + 3, 4)},
        {"z": lax.rem(z + 1, 8)},
        {"z": lax.rem(z + 7, 8)},
        {"h": 1 - h},
        {"l": 1 - low},
        {"f": 1 - core},
    )
    for peer in peers:
        pl.semaphore_signal(barrier, inc=1, device_id=peer, device_id_type=MESH)
    pl.semaphore_wait(barrier, len(peers))

    mine = aligned(core * quarter, quarter)
    theirs = aligned((1 - core) * quarter, quarter)
    leaving = aligned((1 - low) * half + core * quarter, quarter)

    def remote(src, dst, send, recv, peer):
        return pltpu.make_async_remote_copy(
            src_ref=src, dst_ref=dst, send_sem=send, recv_sem=recv, device_id=peer, device_id_type=MESH
        )

    def y_copy(j):
        src = x_hbm.at[leaving, pl.ds(j * width, width)]
        return remote(src, raw.at[j, mine], y_send.at[j], y_recv.at[j], {"l": 1 - low})

    def s_copy(j, rows):
        return remote(raw.at[j, rows], raw.at[j, rows], s_send.at[j], s_recv.at[j], {"f": 1 - core})

    for j in range(4):
        y_copy(j).start()
    loads = load_sem.shape[0]
    block = pairs // loads

    def load(b):
        rows = pl.ds(b * block, block)
        return pltpu.make_async_copy(x_hbm.at[rows], own.at[rows], load_sem.at[b])

    for b in range(loads):
        load(b).start()

    freq = w_ref[0]

    @pl.loop(0, pairs // 128)
    def _(b):
        energy = e_ref[pl.ds(b, 1), :]
        value = jnp.sqrt(4.0 * energy / (energy * energy + freq * freq))
        fac[aligned(b * 128, 128), :] = jnp.broadcast_to(value, (128, 128)).T

    for b in range(loads):
        load(b).wait()

        @pl.loop(0, block // 64)
        def _(i):
            rows = aligned(b * block + i * 64, 64)
            scale = fac[rows, :]
            for c in range(cols // 128):
                lanes = pl.ds(c * 128, 128)
                own[rows, lanes] = (scale * own[rows, lanes].astype(jnp.float32)).astype(jnp.bfloat16)

    ring_d = Ring("z", 8, lambda d, s: d_part.at[d, pl.ds(s * 64, 64)], d_box, d_send, d_recv)
    ring_f = Ring("x", 4, lambda d, s: f_part.at[d, pl.ds(s * 64, 64)], f_box, f_send, f_recv)
    ring_c = [
        Ring("x", 4, lambda d, s, j=j: c_part.at[j, d, pl.ds(s * mid, mid)], c_box.at[j], c_send.at[j], c_recv.at[j])
        for j in range(4)
    ]
    ring_e = [
        Ring("z", 8, lambda d, s, t=t: e_part.at[t, d, pl.ds(s * 64, 64)], e_box.at[t], e_send.at[t], e_recv.at[t])
        for t in range(2)
    ]

    def run(ring, step):
        for way, side, dist in ring.steps()[step]:
            ring.hop(way, side, dist)

    def own_pair(ways):
        first, second = (ring_d.toward(*way) for way in ways)
        lanes = [own[:, aligned(d * 128, 128)] for d in (first, second)]
        block = gram(jnp.concatenate(lanes, axis=1), own[...])
        d_part[first] = block[:128]
        d_part[second] = block[128:]

    mine_half = aligned(low * half, half)

    def cross(j):
        y_copy(j).wait_recv()
        s_copy(j, mine).start()
        s_copy(j, theirs).wait_recv()

        @pl.loop(0, half // 64)
        def _(i):
            rows = aligned(i * 64, 64)
            scale = fac[aligned(low * half + i * 64, 64), :]
            for c in range(width // 128):
                lanes = pl.ds(c * 128, 128)
                other[rows, lanes] = (scale * raw[j, rows, lanes].astype(jnp.float32)).astype(jnp.bfloat16)

        block = gram(other[...], own[mine_half, :])
        for d in range(4):
            c_part[j, d] = block[:, d * width : (d + 1) * width]
        ring_c[j].begin_all()

    def cross_x_done(j):
        ring_c[j].arrived()
        for side in range(2):
            for c in range(2):
                lanes = pl.ds(c * 128, 128)

                @pl.loop(0, mid // 16)
                def _(i):
                    rows = aligned(i * 16, 16)
                    e_part[j // 2, 2 * (2 * (j % 2) + side) + c, rows, :] = (
                        c_part[j, x, aligned(side * mid + i * 16, 16), lanes]
                        + c_box[j, 0, side, 0, rows, lanes]
                        + c_box[j, 1, side, 0, rows, lanes]
                    )

    def h_copy(t):
        return remote(tile.at[t], tile_box, h_send.at[0], h_recv.at[0], {"h": 1 - h})

    def n_copy(q):
        peer = {"x": 2 * (1 - low) + h, "z": 2 * div(z, 2) + q // 2, "h": jnp.int32(q % 2)}
        slot = 2 * x + lax.rem(z, 2)
        own_slot = (peer["x"] == x) & (peer["z"] == z) & (peer["h"] == h)
        return slot, own_slot, remote(
            tile.at[h, pl.ds(32 * q, 32)], in_n.at[slot], out_n_sem.at[q], in_n_sem.at[slot], peer
        )

    def t_copy(q):
        peer = {
            "x": 2 * low + div(x, 2),
            "z": 4 * lax.rem(x, 2) + 2 * lax.rem(z, 2) + q // 2,
            "h": jnp.int32(q % 2),
            "l": 1 - low,
        }
        slot = 4 * h + div(z, 2)
        return remote(
            tile_t.at[pl.ds(32 * q, 32)], in_t.at[slot], out_t_sem.at[q], in_t_sem.at[slot], peer
        )

    def cross_z_done(t):
        ring = ring_e[t]
        ring.arrived()
        for side in range(2):

            @pl.loop(0, 4)
            def _(i):
                rows = aligned(i * 16, 16)
                into = aligned(side * 64 + i * 16, 16)
                tile[t, into, :] = (
                    e_part[t, z, into, :] + e_box[t, 0, side, 0, rows, :] + e_box[t, 1, side, 0, rows, :]
                )

        @pl.when(h != t)
        def _():
            h_copy(t).start()

        @pl.when(h == t)
        def _():
            h_copy(t).wait_recv()
            total = tile[t] + tile_box[...]
            tile[t] = total
            tile_t[...] = total.T
            for q in range(4):
                t_copy(q).start()
                slot, own_slot, copy = n_copy(q)

                @pl.when(jnp.logical_not(own_slot))
                def _():
                    copy.start()

                @pl.when(own_slot)
                def _():
                    in_n[slot] = tile[t, pl.ds(32 * q, 32), :]

    def own_z_done():
        ring_d.arrived()
        for d in range(4):
            lanes = pl.ds(d * width, width)
            for side in range(2):

                @pl.loop(0, 4)
                def _(i):
                    rows = aligned(i * 16, 16)
                    into = aligned(side * 64 + i * 16, 16)
                    f_part[d, into, :] = (
                        d_part[z, into, lanes] + d_box[0, side, 0, rows, lanes] + d_box[1, side, 0, rows, lanes]
                    )
        ring_f.begin_all()

    def dh_copy():
        src = d_tile.at[aligned((1 - h) * 64, 64)]
        return remote(src, d_tile_box, h_send.at[1], h_recv.at[1], {"h": 1 - h})

    def own_x_done():
        ring_f.arrived()
        for side in range(2):

            @pl.loop(0, 4)
            def _(i):
                rows = aligned(i * 16, 16)
                into = aligned(side * 64 + i * 16, 16)
                d_tile[into, :] = f_part[x, into, :] + f_box[0, side, 0, rows, :] + f_box[1, side, 0, rows, :]

        dh_copy().start()

    def od_copy(q):
        peer = {"x": 2 * low + div(z, 4), "z": 2 * lax.rem(z, 4) + h, "h": jnp.int32(q)}
        own_slot = (peer["x"] == x) & (peer["z"] == z) & (peer["h"] == h)
        src = d_tile.at[aligned(h * 64 + 32 * q, 32)]
        return own_slot, remote(src, in_d.at[x], out_d_sem.at[q], in_d_sem.at[x], peer)

    def own_h_done():
        dh_copy().wait_recv()

        @pl.loop(0, 4)
        def _(i):
            into = aligned(h * 64 + i * 16, 16)
            d_tile[into, :] = d_tile[into, :] + d_tile_box[aligned(i * 16, 16), :]

        for q in range(2):
            own_slot, copy = od_copy(q)

            @pl.when(jnp.logical_not(own_slot))
            def _():
                copy.start()

            @pl.when(own_slot)
            def _():
                in_d[x] = d_tile[aligned(h * 64 + 32 * q, 32), :]

    own_pair(((0, 4), (0, 3)))
    ring_d.begin(0, 0)
    ring_d.begin(1, 1)
    ring_d.begin(0, 1)
    own_pair(((1, 3), (0, 2)))
    ring_d.begin(1, 0)
    own_pair(((1, 2), (0, 1)))
    own_pair(((1, 1), (0, 0)))
    cross(0)
    run(ring_d, 0)
    run(ring_c[0], 0)
    cross(1)
    run(ring_d, 1)
    run(ring_c[1], 0)
    cross_x_done(0)
    run(ring_d, 2)
    cross_x_done(1)
    ring_e[0].begin_all()
    cross(2)
    run(ring_d, 3)
    run(ring_c[2], 0)
    run(ring_e[0], 0)
    run(ring_e[0], 1)
    run(ring_e[0], 2)
    cross(3)
    run(ring_e[0], 3)
    run(ring_d, 4)
    run(ring_e[0], 4)
    cross_x_done(2)
    run(ring_c[3], 0)
    cross_z_done(0)
    cross_x_done(3)
    ring_e[1].begin_all()
    run(ring_e[1], 0)
    run(ring_e[1], 1)
    own_z_done()
    run(ring_e[1], 2)
    run(ring_e[1], 3)
    run(ring_f, 0)
    run(ring_e[1], 4)
    cross_z_done(1)
    own_x_done()
    own_h_done()

    @pl.when(div(x, 2) == low)
    def _():
        here = (4 * (x - 2 * low) + div(z, 2) == z) & (lax.rem(z, 2) == h)
        for s in range(4):

            @pl.when(jnp.logical_not(here & (x == s)))
            def _():
                remote(in_d.at[s], in_d.at[s], out_d_sem.at[0], in_d_sem.at[s], {"h": 1 - h}).wait_recv()

            out_ref[:, s * width : (s + 1) * width] = in_d[s]

    @pl.when(div(x, 2) != low)
    def _():
        here = x - 2 * (1 - low) == h
        for s in range(8):

            @pl.when(jnp.logical_not(here & (2 * x + lax.rem(z, 2) == s)))
            def _():
                remote(in_n.at[s], in_n.at[s], out_n_sem.at[0], in_n_sem.at[s], {"h": 1 - h}).wait_recv()

            remote(in_t.at[s], in_t.at[s], out_t_sem.at[0], in_t_sem.at[s], {"h": 1 - h}).wait_recv()
            out_ref[:, s * 128 : (s + 1) * 128] = in_n[s] + in_t[s]

    for j in range(4):
        y_copy(j).wait_send()
        s_copy(j, mine).wait_send()
    for ring in (ring_d, ring_f, *ring_c, *ring_e):
        ring.drain()
    h_copy(1 - h).wait_send()
    dh_copy().wait_send()
    for q in range(4):
        t_copy(q).wait_send()
        _, own_slot, n_out = n_copy(q)

        @pl.when(jnp.logical_not(own_slot))
        def _():
            n_out.wait_send()

    for q in range(2):
        own_slot, d_out = od_copy(q)

        @pl.when(jnp.logical_not(own_slot))
        def _():
            d_out.wait_send()


def per_device(pair_matrix, energies, omega):
    pairs, cols = pair_matrix.shape
    width = cols // 4
    dma = pltpu.SemaphoreType.DMA
    loads = 6

    def f32(*shape):
        return pltpu.VMEM(shape, jnp.float32)

    def bf16(*shape):
        return pltpu.VMEM(shape, jnp.bfloat16)

    owned = pl.pallas_call(
        kernel,
        out_shape=jax.ShapeDtypeStruct((32, cols), jnp.float32),
        in_specs=[
            pl.BlockSpec(memory_space=pltpu.VMEM),
            pl.BlockSpec(memory_space=pltpu.SMEM),
            pl.BlockSpec(memory_space=pl.ANY),
        ],
        out_specs=pl.BlockSpec(memory_space=pltpu.VMEM),
        scratch_shapes=[
            bf16(pairs, cols),
            f32(pairs, 128),
            bf16(4, pairs // 2, width),
            bf16(pairs // 2, width),
            f32(8, 128, cols),
            f32(2, 2, 4, 64, cols),
            f32(4, 4, width, width),
            f32(4, 2, 2, 2, width // 2, width),
            f32(2, 8, 128, 128),
            f32(2, 2, 2, 4, 64, 128),
            f32(4, 128, width),
            f32(2, 2, 2, 64, width),
            f32(2, 128, 128),
            f32(128, 128),
            f32(128, 128),
            f32(128, width),
            f32(64, width),
            f32(4, 32, width),
            f32(8, 32, 128),
            f32(8, 32, 128),
            dma((loads,)),
            dma((4,)),
            dma((4,)),
            dma((4,)),
            dma((4,)),
            dma((2, 2, 4)),
            dma((2, 2, 4)),
            dma((4, 2, 2, 2)),
            dma((4, 2, 2, 2)),
            dma((2, 2, 2, 4)),
            dma((2, 2, 2, 4)),
            dma((2, 2, 2)),
            dma((2, 2, 2)),
            dma((2,)),
            dma((2,)),
            dma((4,)),
            dma((8,)),
            dma((8,)),
            dma((2,)),
            dma((4,)),
            dma((4,)),
        ],
        compiler_params=pltpu.CompilerParams(
            collective_id=0, has_side_effects=True, vmem_limit_bytes=60 * 1024 * 1024
        ),
    )(energies.reshape(pairs // 128, 128), omega, pair_matrix)
    return owned[:, None, :]


def solution(mesh):
    finer = Mesh(mesh.devices.reshape(4, 8, 2, 2, 2), ("x", "z", "h", "l", "f"))
    return jax.shard_map(
        per_device,
        mesh=finer,
        in_specs=(P(ROWS, "l"), P(ROWS), P("f")),
        out_specs=P(ROWS, "f", "l"),
        check_vma=False,
    )
```

time: 365 us -> 107 us (0.29)
  the two profiles are of different devices: /device:TPU:6 before, /device:TPU:18 now
where the time goes in v2:
time: 107 us
  Pallas kernels  105 us (98%)
  local copies, waits for them, and re-layouts  1.69 us (2%)
    pallas_call x1, Pallas kernels, per_device(): pl.pallas_call(kernel, out_shape=jax.ShapeDtypeStruct((32, cols), jnp.flo...  105 us

profile of v2, /device:TPU:18, one launch (start us, length us, event | category | flops | bytes accessed | tf_op | source)
XLA Modules:
  0.0 107.2 jit_solution(5738273886368383723)
XLA Ops:
  0.7 104.9 %shard_map.37 = f32[32,1024]{1,0:T(8,128)} custom-call(f32[24,128]{1,0:T(8,128)} %bitcast.3, f32[1]{0:T(128)S(6)} %copy.5.w_ref, bf16[3072,1024]{1,0:T(8,128)(2,1)} %x_hbm.1), custom_call_target="tpu_custom_call" | custom-call | tf_op jit(solution)/shard_map/pallas_call | solution.py:472
  105.5 1.7 %copy.4 = f32[32,1,1024]{2,1,0:T(1,128)} copy(f32[32,1,1024]{2,0,1:T(8,128)} %bitcast.2) | data formatting | bytes 262144 | tf_op jit(solution)/shard_map/broadcast_in_dim | solution.py:528

commit v3 on v2

--- a/solution.py
+++ b/solution.py
@@ -8,6 +8,7 @@
 
 MESH = pl.DeviceIdType.MESH
 ROWS = ("x", "z", "h")
+CHUNKS = ((0, 256), (256, 256), (512, 256), (768, 128), (896, 128))
 
 
 def gram(left, right):
@@ -16,8 +17,8 @@
     )
 
 
-def aligned(value, size):
-    return pl.ds(pl.multiple_of(value, size), size)
+def aligned(value, size, length=None):
+    return pl.ds(pl.multiple_of(value, size), length or size)
 
 
 class Ring:
@@ -35,7 +36,7 @@
     def copy(self, way, side, dist):
         return pltpu.make_async_remote_copy(
             src_ref=self.block(self.toward(way, dist), side),
-            dst_ref=self.inbox.at[way, side, dist - 1],
+            dst_ref=self.inbox(way, side, dist - 1),
             send_sem=self.send_sem.at[way, side, dist - 1],
             recv_sem=self.recv_sem.at[way, side, dist - 1],
             device_id={self.axis: self.toward(way, 1)},
@@ -48,7 +49,7 @@
     def hop(self, way, side, dist):
         self.copy(way, side, dist + 1).wait_recv()
         held = self.block(self.toward(way, dist), side)
-        came = self.inbox.at[way, side, dist]
+        came = self.inbox(way, side, dist)
 
         @pl.loop(0, held.shape[0] // 16)
         def _(i):
@@ -101,9 +102,13 @@
     tile,
     tile_t,
     tile_box,
-    d_tile,
-    d_tile_box,
+    d_sum,
+    d_sum_box,
+    d_fin,
+    pad,
+    turned,
     in_d,
+    in_dt,
     in_n,
     in_t,
     load_sem,
@@ -122,17 +127,20 @@
     h_send,
     h_recv,
     in_d_sem,
+    in_dt_sem,
     in_n_sem,
     in_t_sem,
     out_d_sem,
+    out_dt_sem,
     out_n_sem,
     out_t_sem,
 ):
     x, z, h = lax.axis_index("x"), lax.axis_index("z"), lax.axis_index("h")
     low, core = lax.axis_index("l"), lax.axis_index("f")
-    pairs, cols = own.shape
+    pairs, cols = x_hbm.shape
     half, width = pairs // 2, cols // 4
-    quarter, mid = half // 2, width // 2
+    quarter = half // 2
+    wide = d_part.shape[2]
     div = lax.div
 
     barrier = pltpu.get_barrier_semaphore()
@@ -159,20 +167,20 @@
         )
 
     def y_copy(j):
-        src = x_hbm.at[leaving, pl.ds(j * width, width)]
-        return remote(src, raw.at[j, mine], y_send.at[j], y_recv.at[j], {"l": 1 - low})
+        src = x_hbm.at[leaving, pl.ds(*CHUNKS[j])]
+        return remote(src, raw[j].at[mine], y_send.at[j], y_recv.at[j], {"l": 1 - low})
 
     def s_copy(j, rows):
-        return remote(raw.at[j, rows], raw.at[j, rows], s_send.at[j], s_recv.at[j], {"f": 1 - core})
-
-    for j in range(4):
+        return remote(raw[j].at[rows], raw[j].at[rows], s_send.at[j], s_recv.at[j], {"f": 1 - core})
+
+    for j in range(len(CHUNKS)):
         y_copy(j).start()
     loads = load_sem.shape[0]
     block = pairs // loads
 
     def load(b):
         rows = pl.ds(b * block, block)
-        return pltpu.make_async_copy(x_hbm.at[rows], own.at[rows], load_sem.at[b])
+        return pltpu.make_async_copy(x_hbm.at[rows], own.at[rows, pl.ds(0, cols)], load_sem.at[b])
 
     for b in range(loads):
         load(b).start()
@@ -194,16 +202,40 @@
             scale = fac[rows, :]
             for c in range(cols // 128):
                 lanes = pl.ds(c * 128, 128)
-                own[rows, lanes] = (scale * own[rows, lanes].astype(jnp.float32)).astype(jnp.bfloat16)
-
-    ring_d = Ring("z", 8, lambda d, s: d_part.at[d, pl.ds(s * 64, 64)], d_box, d_send, d_recv)
-    ring_f = Ring("x", 4, lambda d, s: f_part.at[d, pl.ds(s * 64, 64)], f_box, f_send, f_recv)
-    ring_c = [
-        Ring("x", 4, lambda d, s, j=j: c_part.at[j, d, pl.ds(s * mid, mid)], c_box.at[j], c_send.at[j], c_recv.at[j])
-        for j in range(4)
-    ]
+                scaled = (scale * own[rows, lanes].astype(jnp.float32)).astype(jnp.bfloat16)
+                own[rows, lanes] = scaled
+                if c < 5:
+                    own[rows, pl.ds(cols + c * 128, 128)] = scaled
+
+    ring_d = Ring(
+        "z", 8, lambda d, s: d_part.at[d, pl.ds(s * 64, 64)], lambda *i: d_box.at[*i], d_send, d_recv
+    )
+    ring_f = Ring(
+        "x", 4, lambda d, s: f_part.at[d, pl.ds(s * 16, 16)], lambda *i: f_box.at[*i], f_send, f_recv
+    )
+
+    def ring_of_chunk(j):
+        first, size = CHUNKS[j]
+        mid = size // 2
+
+        def block(d, s):
+            return c_part.at[d, pl.ds(first + s * mid, mid)]
+
+        def inbox(way, side, k):
+            return c_box.at[way, side, k, pl.ds(first // 2, mid)]
+
+        return Ring("x", 4, block, inbox, c_send.at[j], c_recv.at[j])
+
+    ring_c = [ring_of_chunk(j) for j in range(len(CHUNKS))]
     ring_e = [
-        Ring("z", 8, lambda d, s, t=t: e_part.at[t, d, pl.ds(s * 64, 64)], e_box.at[t], e_send.at[t], e_recv.at[t])
+        Ring(
+            "z",
+            8,
+            lambda d, s, t=t: e_part.at[t, d, pl.ds(s * 64, 64)],
+            lambda *i, t=t: e_box.at[t, *i],
+            e_send.at[t],
+            e_recv.at[t],
+        )
         for t in range(2)
     ]
 
@@ -211,16 +243,17 @@
         for way, side, dist in ring.steps()[step]:
             ring.hop(way, side, dist)
 
-    def own_pair(ways):
-        first, second = (ring_d.toward(*way) for way in ways)
-        lanes = [own[:, aligned(d * 128, 128)] for d in (first, second)]
-        block = gram(jnp.concatenate(lanes, axis=1), own[...])
-        d_part[first] = block[:128]
-        d_part[second] = block[128:]
+    def own_pair(way, dist):
+        one = ring_d.toward(way, dist)
+        two = lax.rem(one + 1, 8)
+        block = gram(own[:, aligned(one * 128, 128, 256)], own[:, aligned(one * 128, 128, wide + 128)])
+        d_part[one] = block[:128, :wide]
+        d_part[two] = block[128:, 128:]
 
     mine_half = aligned(low * half, half)
 
     def cross(j):
+        first, size = CHUNKS[j]
         y_copy(j).wait_recv()
         s_copy(j, mine).start()
         s_copy(j, theirs).wait_recv()
@@ -229,28 +262,31 @@
         def _(i):
             rows = aligned(i * 64, 64)
             scale = fac[aligned(low * half + i * 64, 64), :]
-            for c in range(width // 128):
+            for c in range(size // 128):
                 lanes = pl.ds(c * 128, 128)
-                other[rows, lanes] = (scale * raw[j, rows, lanes].astype(jnp.float32)).astype(jnp.bfloat16)
-
-        block = gram(other[...], own[mine_half, :])
+                other[rows, lanes] = (scale * raw[j][rows, lanes].astype(jnp.float32)).astype(jnp.bfloat16)
+
+        block = gram(other[:, :size], own[mine_half, :cols])
         for d in range(4):
-            c_part[j, d] = block[:, d * width : (d + 1) * width]
+            c_part[d, pl.ds(first, size), :] = block[:, d * width : (d + 1) * width]
         ring_c[j].begin_all()
 
     def cross_x_done(j):
+        first, size = CHUNKS[j]
+        mid = size // 2
         ring_c[j].arrived()
         for side in range(2):
+            start = first + side * mid
             for c in range(2):
                 lanes = pl.ds(c * 128, 128)
 
                 @pl.loop(0, mid // 16)
                 def _(i):
-                    rows = aligned(i * 16, 16)
-                    e_part[j // 2, 2 * (2 * (j % 2) + side) + c, rows, :] = (
-                        c_part[j, x, aligned(side * mid + i * 16, 16), lanes]
-                        + c_box[j, 0, side, 0, rows, lanes]
-                        + c_box[j, 1, side, 0, rows, lanes]
+                    rows = aligned(first // 2 + i * 16, 16)
+                    e_part[start // 512, 2 * (start % 512 // 128) + c, aligned(start % 128 + i * 16, 16), :] = (
+                        c_part[x, aligned(start + i * 16, 16), lanes]
+                        + c_box[0, side, 0, rows, lanes]
+                        + c_box[1, side, 0, rows, lanes]
                     )
 
     def h_copy(t):
@@ -313,114 +349,142 @@
 
     def own_z_done():
         ring_d.arrived()
-        for d in range(4):
-            lanes = pl.ds(d * width, width)
-            for side in range(2):
-
-                @pl.loop(0, 4)
+        for side in range(2):
+            for part in range(2):
+                d = 2 * side + part
+
+                @pl.loop(0, 2)
                 def _(i):
-                    rows = aligned(i * 16, 16)
-                    into = aligned(side * 64 + i * 16, 16)
-                    f_part[d, into, :] = (
-                        d_part[z, into, lanes] + d_box[0, side, 0, rows, lanes] + d_box[1, side, 0, rows, lanes]
+                    rows = aligned(part * 32 + i * 16, 16)
+                    f_part[d, aligned(i * 16, 16), :] = (
+                        d_part[z, aligned(d * 32 + i * 16, 16), :]
+                        + d_box[0, side, 0, rows, :]
+                        + d_box[1, side, 0, rows, :]
                     )
+
         ring_f.begin_all()
 
     def dh_copy():
-        src = d_tile.at[aligned((1 - h) * 64, 64)]
-        return remote(src, d_tile_box, h_send.at[1], h_recv.at[1], {"h": 1 - h})
+        return remote(d_sum, d_sum_box, h_send.at[1], h_recv.at[1], {"h": 1 - h})
 
     def own_x_done():
         ring_f.arrived()
         for side in range(2):
-
-            @pl.loop(0, 4)
-            def _(i):
-                rows = aligned(i * 16, 16)
-                into = aligned(side * 64 + i * 16, 16)
-                d_tile[into, :] = f_part[x, into, :] + f_box[0, side, 0, rows, :] + f_box[1, side, 0, rows, :]
-
+            rows = pl.ds(side * 16, 16)
+            d_sum[rows, :] = f_part[x, rows, :] + f_box[0, side, 0] + f_box[1, side, 0]
         dh_copy().start()
 
-    def od_copy(q):
-        peer = {"x": 2 * low + div(z, 4), "z": 2 * lax.rem(z, 4) + h, "h": jnp.int32(q)}
-        own_slot = (peer["x"] == x) & (peer["z"] == z) & (peer["h"] == h)
-        src = d_tile.at[aligned(h * 64 + 32 * q, 32)]
-        return own_slot, remote(src, in_d.at[x], out_d_sem.at[q], in_d_sem.at[x], peer)
+    def straight_copy():
+        peer = {"x": 2 * low + div(z, 4), "z": 2 * lax.rem(z, 4) + div(x, 2)}
+        stays = (peer["x"] == x) & (peer["z"] == z)
+        return stays, remote(d_fin, in_d, out_d_sem.at[0], in_d_sem.at[0], peer)
+
+    def turned_copy(t, k):
+        j = lax.rem(z + t, 8)
+        peer = {"x": 2 * low + div(j, 4), "z": 2 * lax.rem(j, 4) + k}
+        stays = (peer["x"] == x) & (peer["z"] == z)
+        src = turned.at[t - 1, aligned(64 * k + 32 * h, 32)]
+        return stays, src, remote(src, in_dt.at[t - 1, x], out_dt_sem.at[t - 1, k], in_dt_sem.at[t - 1, x], peer)
 
     def own_h_done():
         dh_copy().wait_recv()
-
-        @pl.loop(0, 4)
-        def _(i):
-            into = aligned(h * 64 + i * 16, 16)
-            d_tile[into, :] = d_tile[into, :] + d_tile_box[aligned(i * 16, 16), :]
-
-        for q in range(2):
-            own_slot, copy = od_copy(q)
-
-            @pl.when(jnp.logical_not(own_slot))
+        d_fin[...] = d_sum[...] + d_sum_box[...]
+
+        @pl.when(h == lax.rem(x, 2))
+        def _():
+            stays, copy = straight_copy()
+
+            @pl.when(jnp.logical_not(stays))
             def _():
                 copy.start()
 
-            @pl.when(own_slot)
+            @pl.when(stays)
             def _():
-                in_d[x] = d_tile[aligned(h * 64 + 32 * q, 32), :]
-
-    own_pair(((0, 4), (0, 3)))
+                in_d[...] = d_fin[...]
+
+        pad[...] = jnp.zeros_like(pad)
+        for t in range(1, 4):
+            pad[aligned(x * 32, 32), :] = d_fin[:, t * 128 : (t + 1) * 128]
+            turned[t - 1] = pad[...].T
+            for k in range(2):
+                stays, src, copy = turned_copy(t, k)
+
+                @pl.when(jnp.logical_not(stays))
+                def _():
+                    copy.start()
+
+                @pl.when(stays)
+                def _():
+                    in_dt[t - 1, x] = src[...]
+
+    own_pair(0, 3)
     ring_d.begin(0, 0)
     ring_d.begin(1, 1)
     ring_d.begin(0, 1)
-    own_pair(((1, 3), (0, 2)))
+    own_pair(1, 3)
     ring_d.begin(1, 0)
-    own_pair(((1, 2), (0, 1)))
-    own_pair(((1, 1), (0, 0)))
+    own_pair(0, 1)
+    own_pair(1, 1)
     cross(0)
     run(ring_d, 0)
+    run(ring_d, 1)
     run(ring_c[0], 0)
     cross(1)
-    run(ring_d, 1)
+    run(ring_d, 2)
+    run(ring_d, 3)
+    cross_x_done(0)
     run(ring_c[1], 0)
-    cross_x_done(0)
-    run(ring_d, 2)
+    run(ring_d, 4)
+    cross(2)
     cross_x_done(1)
     ring_e[0].begin_all()
-    cross(2)
-    run(ring_d, 3)
+    cross(3)
     run(ring_c[2], 0)
     run(ring_e[0], 0)
+    own_z_done()
+    cross(4)
+    run(ring_c[3], 0)
     run(ring_e[0], 1)
+    run(ring_f, 0)
+    cross_x_done(2)
     run(ring_e[0], 2)
-    cross(3)
+    run(ring_c[4], 0)
+    cross_x_done(3)
     run(ring_e[0], 3)
-    run(ring_d, 4)
+    own_x_done()
+    cross_x_done(4)
+    ring_e[1].begin_all()
     run(ring_e[0], 4)
-    cross_x_done(2)
-    run(ring_c[3], 0)
+    own_h_done()
+    run(ring_e[1], 0)
     cross_z_done(0)
-    cross_x_done(3)
-    ring_e[1].begin_all()
-    run(ring_e[1], 0)
-    run(ring_e[1], 1)
-    own_z_done()
-    run(ring_e[1], 2)
-    run(ring_e[1], 3)
-    run(ring_f, 0)
-    run(ring_e[1], 4)
+    for step in range(1, 5):
+        run(ring_e[1], step)
     cross_z_done(1)
-    own_x_done()
-    own_h_done()
 
     @pl.when(div(x, 2) == low)
     def _():
-        here = (4 * (x - 2 * low) + div(z, 2) == z) & (lax.rem(z, 2) == h)
-        for s in range(4):
-
-            @pl.when(jnp.logical_not(here & (x == s)))
-            def _():
-                remote(in_d.at[s], in_d.at[s], out_d_sem.at[0], in_d_sem.at[s], {"h": 1 - h}).wait_recv()
-
-            out_ref[:, s * width : (s + 1) * width] = in_d[s]
+        j = 4 * (x - 2 * low) + div(z, 2)
+        p = 2 * lax.rem(z, 2) + h
+
+        @pl.when(jnp.logical_not((z == j) & (x == p)))
+        def _():
+            remote(in_d, in_d, out_d_sem.at[0], in_d_sem.at[0], {"h": 1 - h}).wait_recv()
+
+        for t in range(5):
+            out_ref[:, aligned(lax.rem(j + t, 8) * 128, 128)] = in_d[:, t * 128 : (t + 1) * 128]
+        for t in range(1, 4):
+            source = lax.rem(j + 8 - t, 8)
+            for q in range(4):
+
+                @pl.when(jnp.logical_not((z == source) & (x == q)))
+                def _():
+                    box = in_dt.at[t - 1, q]
+                    remote(box, box, out_dt_sem.at[0, 0], in_dt_sem.at[t - 1, q], {"h": 1 - h}).wait_recv()
+
+            out_ref[:, aligned(source * 128, 128)] = (
+                in_dt[t - 1, 0] + in_dt[t - 1, 1] + in_dt[t - 1, 2] + in_dt[t - 1, 3]
+            )
 
     @pl.when(div(x, 2) != low)
     def _():
@@ -434,7 +498,7 @@
             remote(in_t.at[s], in_t.at[s], out_t_sem.at[0], in_t_sem.at[s], {"h": 1 - h}).wait_recv()
             out_ref[:, s * 128 : (s + 1) * 128] = in_n[s] + in_t[s]
 
-    for j in range(4):
+    for j in range(len(CHUNKS)):
         y_copy(j).wait_send()
         s_copy(j, mine).wait_send()
     for ring in (ring_d, ring_f, *ring_c, *ring_e):
@@ -449,19 +513,26 @@
         def _():
             n_out.wait_send()
 
-    for q in range(2):
-        own_slot, d_out = od_copy(q)
-
-        @pl.when(jnp.logical_not(own_slot))
-        def _():
-            d_out.wait_send()
+    stays, straight = straight_copy()
+
+    @pl.when((h == lax.rem(x, 2)) & jnp.logical_not(stays))
+    def _():
+        straight.wait_send()
+
+    for t in range(1, 4):
+        for k in range(2):
+            kept, _, turn = turned_copy(t, k)
+
+            @pl.when(jnp.logical_not(kept))
+            def _():
+                turn.wait_send()
 
 
 def per_device(pair_matrix, energies, omega):
     pairs, cols = pair_matrix.shape
     width = cols // 4
     dma = pltpu.SemaphoreType.DMA
-    loads = 6
+    loads, chunks = 6, len(CHUNKS)
 
     def f32(*shape):
         return pltpu.VMEM(shape, jnp.float32)
@@ -479,45 +550,51 @@
         ],
         out_specs=pl.BlockSpec(memory_space=pltpu.VMEM),
         scratch_shapes=[
-            bf16(pairs, cols),
+            bf16(pairs, 13 * 128),
             f32(pairs, 128),
-            bf16(4, pairs // 2, width),
+            [bf16(pairs // 2, size) for _, size in CHUNKS],
             bf16(pairs // 2, width),
-            f32(8, 128, cols),
-            f32(2, 2, 4, 64, cols),
-            f32(4, 4, width, width),
-            f32(4, 2, 2, 2, width // 2, width),
+            f32(8, 128, 640),
+            f32(2, 2, 4, 64, 640),
+            f32(4, cols, width),
+            f32(2, 2, 2, cols // 2, width),
             f32(2, 8, 128, 128),
             f32(2, 2, 2, 4, 64, 128),
-            f32(4, 128, width),
-            f32(2, 2, 2, 64, width),
+            f32(4, 32, 640),
+            f32(2, 2, 2, 16, 640),
             f32(2, 128, 128),
             f32(128, 128),
             f32(128, 128),
-            f32(128, width),
-            f32(64, width),
-            f32(4, 32, width),
+            f32(32, 640),
+            f32(32, 640),
+            f32(32, 640),
+            f32(128, 128),
+            f32(3, 128, 128),
+            f32(32, 640),
+            f32(3, 4, 32, 128),
             f32(8, 32, 128),
             f32(8, 32, 128),
             dma((loads,)),
-            dma((4,)),
-            dma((4,)),
-            dma((4,)),
-            dma((4,)),
+            dma((chunks,)),
+            dma((chunks,)),
+            dma((chunks,)),
+            dma((chunks,)),
             dma((2, 2, 4)),
             dma((2, 2, 4)),
-            dma((4, 2, 2, 2)),
-            dma((4, 2, 2, 2)),
+            dma((chunks, 2, 2, 2)),
+            dma((chunks, 2, 2, 2)),
             dma((2, 2, 2, 4)),
             dma((2, 2, 2, 4)),
             dma((2, 2, 2)),
             dma((2, 2, 2)),
             dma((2,)),
             dma((2,)),
-            dma((4,)),
+            dma((1,)),
+            dma((3, 4)),
             dma((8,)),
             dma((8,)),
-            dma((2,)),
+            dma((1,)),
+            dma((3, 2)),
             dma((4,)),
             dma((4,)),
         ],

time: 107 us -> 96.2 us (0.90)
  the two profiles are of different devices: /device:TPU:18 before, /device:TPU:6 now
where the time goes in v3:
time: 96.2 us; the launch traced here: 95.6 us
  Pallas kernels  93.2 us (97%)
  local copies, waits for them, and re-layouts  1.69 us (2%)
    pallas_call x1, Pallas kernels, per_device(): pl.pallas_call(kernel, out_shape=jax.ShapeDtypeStruct((32, cols), jnp.flo...  93.2 us

profile of v3, /device:TPU:6, one launch (start us, length us, event | category | flops | bytes accessed | tf_op | source)
XLA Modules:
  0.0 95.6 jit_solution(17773601844379438415)
XLA Ops:
  0.7 93.2 %shard_map.37 = f32[32,1024]{1,0:T(8,128)} custom-call(f32[24,128]{1,0:T(8,128)} %bitcast.3, f32[1]{0:T(128)S(6)} %copy.5.w_ref, bf16[3072,1024]{1,0:T(8,128)(2,1)} %x_hbm.1), custom_call_target="tpu_custom_call" | custom-call | tf_op jit(solution)/shard_map/pallas_call | solution.py:543
  93.9 1.7 %copy.4 = f32[32,1,1024]{2,1,0:T(1,128)} copy(f32[32,1,1024]{2,0,1:T(8,128)} %bitcast.2) | data formatting | bytes 262144 | tf_op jit(solution)/shard_map/broadcast_in_dim | solution.py:605

commit v4 on v3

--- a/solution.py
+++ b/solution.py
@@ -80,6 +80,56 @@
             for side in range(2):
                 for dist in range(self.first(way, side), 0, -1):
                     self.copy(way, side, dist).wait_send()
+
+
+class CodedRing(Ring):
+    def __init__(self, *ring, staged, scale):
+        super().__init__(*ring)
+        self.staged, (self.enc, self.dec) = staged, scale
+
+    def copy(self, way, side, dist):
+        return pltpu.make_async_remote_copy(
+            src_ref=self.staged(way, side, dist - 1),
+            dst_ref=self.inbox(way, side, dist - 1),
+            send_sem=self.send_sem.at[way, side, dist - 1],
+            recv_sem=self.recv_sem.at[way, side, dist - 1],
+            device_id={self.axis: self.toward(way, 1)},
+            device_id_type=MESH,
+        )
+
+    def encode(self, value):
+        scaled = value * self.enc[:1, : value.shape[1]]
+        power = scaled * scaled
+        power = power * power
+        power = power * power
+        return jnp.where(scaled < 0, -power, power).astype(jnp.bfloat16)
+
+    def decode(self, code):
+        power = code.astype(jnp.float32)
+        fourth = lax.rsqrt(lax.rsqrt(jnp.maximum(jnp.abs(power), 1e-37)))
+        root = fourth * lax.rsqrt(fourth) * self.dec[:1, : code.shape[1]]
+        return jnp.where(power < 0, -root, root)
+
+    def stage(self, way, side, dist, came=None):
+        held = self.block(self.toward(way, dist), side)
+        staged = self.staged(way, side, dist - 1)
+
+        @pl.loop(0, held.shape[0] // 64)
+        def _(i):
+            rows = aligned(i * 64, 64)
+            value = held[rows, :]
+            if came is not None:
+                value = value + self.decode(came[rows, :])
+            staged[rows, :] = self.encode(value)
+
+        self.copy(way, side, dist).start()
+
+    def begin(self, way, side):
+        self.stage(way, side, self.first(way, side))
+
+    def hop(self, way, side, dist):
+        self.copy(way, side, dist + 1).wait_recv()
+        self.stage(way, side, dist, self.inbox(way, side, dist))
 
 
 def kernel(
@@ -95,6 +145,13 @@
     d_box,
     c_part,
     c_box,
+    c_code,
+    b_own,
+    b_low,
+    b_both,
+    b_far,
+    enc,
+    dec,
     e_part,
     e_box,
     f_part,
@@ -120,6 +177,8 @@
     d_recv,
     c_send,
     c_recv,
+    b_send,
+    b_recv,
     e_send,
     e_recv,
     f_send,
@@ -146,7 +205,9 @@
     barrier = pltpu.get_barrier_semaphore()
     peers = (
         {"x": lax.rem(x + 1, 4)},
+        {"x": lax.rem(x + 2, 4)},
         {"x": lax.rem(x + 3, 4)},
+        {"x": lax.rem(x + 3, 4), "l": 1 - low},
         {"z": lax.rem(z + 1, 8)},
         {"z": lax.rem(z + 7, 8)},
         {"h": 1 - h},
@@ -224,7 +285,12 @@
         def inbox(way, side, k):
             return c_box.at[way, side, k, pl.ds(first // 2, mid)]
 
-        return Ring("x", 4, block, inbox, c_send.at[j], c_recv.at[j])
+        def staged(way, side, k):
+            return c_code.at[way, side, k, pl.ds(first // 2, mid)]
+
+        return CodedRing(
+            "x", 4, block, inbox, c_send.at[j], c_recv.at[j], staged=staged, scale=(enc, dec)
+        )
 
     ring_c = [ring_of_chunk(j) for j in range(len(CHUNKS))]
     ring_e = [
@@ -269,7 +335,34 @@
         block = gram(other[:, :size], own[mine_half, :cols])
         for d in range(4):
             c_part[d, pl.ds(first, size), :] = block[:, d * width : (d + 1) * width]
-        ring_c[j].begin_all()
+
+    def b_copy(k):
+        if k == 0:
+            return remote(b_own, b_low, b_send.at[0], b_recv.at[0], {"x": lax.rem(x + 1, 4), "l": 1 - low})
+        return remote(b_both, b_far.at[k - 1], b_send.at[k], b_recv.at[k], {"x": lax.rem(x + k, 4)})
+
+    def bound_own():
+        most = jnp.abs(d_part[0, :, :128])
+        for d in range(1, 8):
+            most = jnp.maximum(most, jnp.abs(d_part[d, :, :128]))
+        b_own[...] = jnp.full(b_own.shape, jnp.max(most), jnp.float32)
+        b_copy(0).start()
+
+    def bound_both():
+        b_copy(0).wait_recv()
+        b_both[...] = jnp.maximum(b_own[...], b_low[...])
+        for k in range(1, 4):
+            b_copy(k).start()
+
+    def bound_all():
+        most = b_both[...]
+        for k in range(1, 4):
+            b_copy(k).wait_recv()
+            most = jnp.maximum(most, b_far[k - 1])
+        most = jnp.broadcast_to(4.0 * jnp.maximum(most[:1, :], 1e-30), (8, 128))
+        for c in range(2):
+            enc[:, c * 128 : (c + 1) * 128] = 32768.0 / most
+            dec[:, c * 128 : (c + 1) * 128] = most / 32768.0
 
     def cross_x_done(j):
         first, size = CHUNKS[j]
@@ -280,13 +373,13 @@
             for c in range(2):
                 lanes = pl.ds(c * 128, 128)
 
-                @pl.loop(0, mid // 16)
+                @pl.loop(0, mid // 64)
                 def _(i):
-                    rows = aligned(first // 2 + i * 16, 16)
-                    e_part[start // 512, 2 * (start % 512 // 128) + c, aligned(start % 128 + i * 16, 16), :] = (
-                        c_part[x, aligned(start + i * 16, 16), lanes]
-                        + c_box[0, side, 0, rows, lanes]
-                        + c_box[1, side, 0, rows, lanes]
+                    rows = aligned(first // 2 + i * 64, 64)
+                    e_part[start // 512, 2 * (start % 512 // 128) + c, aligned(start % 128 + i * 64, 64), :] = (
+                        c_part[x, aligned(start + i * 64, 64), lanes]
+                        + ring_c[j].decode(c_box[0, side, 0, rows, lanes])
+                        + ring_c[j].decode(c_box[1, side, 0, rows, lanes])
                     )
 
     def h_copy(t):
@@ -425,41 +518,51 @@
     ring_d.begin(1, 0)
     own_pair(0, 1)
     own_pair(1, 1)
+    bound_own()
     cross(0)
+    bound_both()
     run(ring_d, 0)
+    bound_all()
+    ring_c[0].begin_all()
     run(ring_d, 1)
     run(ring_c[0], 0)
     cross(1)
+    ring_c[1].begin_all()
     run(ring_d, 2)
+    cross_x_done(0)
     run(ring_d, 3)
-    cross_x_done(0)
     run(ring_c[1], 0)
     run(ring_d, 4)
     cross(2)
+    ring_c[2].begin_all()
     cross_x_done(1)
     ring_e[0].begin_all()
+    own_z_done()
     cross(3)
+    ring_c[3].begin_all()
     run(ring_c[2], 0)
     run(ring_e[0], 0)
-    own_z_done()
+    run(ring_f, 0)
     cross(4)
+    ring_c[4].begin_all()
     run(ring_c[3], 0)
+    cross_x_done(2)
     run(ring_e[0], 1)
-    run(ring_f, 0)
-    cross_x_done(2)
-    run(ring_e[0], 2)
     run(ring_c[4], 0)
+    own_x_done()
     cross_x_done(3)
-    run(ring_e[0], 3)
-    own_x_done()
     cross_x_done(4)
     ring_e[1].begin_all()
+    run(ring_e[0], 2)
+    run(ring_e[1], 0)
+    own_h_done()
+    run(ring_e[0], 3)
+    run(ring_e[1], 1)
     run(ring_e[0], 4)
-    own_h_done()
-    run(ring_e[1], 0)
+    run(ring_e[1], 2)
     cross_z_done(0)
-    for step in range(1, 5):
-        run(ring_e[1], step)
+    run(ring_e[1], 3)
+    run(ring_e[1], 4)
     cross_z_done(1)
 
     @pl.when(div(x, 2) == low)
@@ -504,6 +607,8 @@
     for ring in (ring_d, ring_f, *ring_c, *ring_e):
         ring.drain()
     h_copy(1 - h).wait_send()
+    for k in range(4):
+        b_copy(k).wait_send()
     dh_copy().wait_send()
     for q in range(4):
         t_copy(q).wait_send()
@@ -557,7 +662,14 @@
             f32(8, 128, 640),
             f32(2, 2, 4, 64, 640),
             f32(4, cols, width),
-            f32(2, 2, 2, cols // 2, width),
+            bf16(2, 2, 2, cols // 2, width),
+            bf16(2, 2, 2, cols // 2, width),
+            f32(8, 128),
+            f32(8, 128),
+            f32(8, 128),
+            f32(3, 8, 128),
+            f32(8, width),
+            f32(8, width),
             f32(2, 8, 128, 128),
             f32(2, 2, 2, 4, 64, 128),
             f32(4, 32, 640),
@@ -583,6 +695,8 @@
             dma((2, 2, 4)),
             dma((chunks, 2, 2, 2)),
             dma((chunks, 2, 2, 2)),
+            dma((4,)),
+            dma((4,)),
             dma((2, 2, 2, 4)),
             dma((2, 2, 2, 4)),
             dma((2, 2, 2)),

time: 96.2 us -> 93.7 us (0.974)
  Pallas kernels: 93.2 us -> 91.2 us
    pallas_call x1, Pallas kernels: 93.2 us -> 91.2 us  [per_device(): pl.pallas_call(kernel, out_shape=jax.ShapeDtypeStruct((32, cols), jnp.flo...]
where the time goes in v4:
time: 93.7 us; the launch traced here: 93.5 us
  Pallas kernels  91.2 us (97%)
  local copies, waits for them, and re-layouts  1.69 us (2%)
    pallas_call x1, Pallas kernels, per_device(): pl.pallas_call(kernel, out_shape=jax.ShapeDtypeStruct((32, cols), jnp.flo...  91.2 us

profile of v4, /device:TPU:6, one launch (start us, length us, event | category | flops | bytes accessed | tf_op | source)
XLA Modules:
  0.0 93.5 jit_solution(10994735866242484916)
XLA Ops:
  0.7 91.2 %shard_map.37 = f32[32,1024]{1,0:T(8,128)} custom-call(f32[24,128]{1,0:T(8,128)} %bitcast.3, f32[1]{0:T(128)S(6)} %copy.5.w_ref, bf16[3072,1024]{1,0:T(8,128)(2,1)} %x_hbm.1), custom_call_target="tpu_custom_call" | custom-call | tf_op jit(solution)/shard_map/pallas_call | solution.py:648
  91.8 1.7 %copy.4 = f32[32,1,1024]{2,1,0:T(1,128)} copy(f32[32,1,1024]{2,0,1:T(8,128)} %bitcast.2) | data formatting | bytes 262144 | tf_op jit(solution)/shard_map/broadcast_in_dim | solution.py:719

commit v5 on v4

--- a/solution.py
+++ b/solution.py
@@ -158,7 +158,6 @@
     f_box,
     tile,
     tile_t,
-    tile_box,
     d_sum,
     d_sum_box,
     d_fin,
@@ -382,27 +381,24 @@
                         + ring_c[j].decode(c_box[1, side, 0, rows, lanes])
                     )
 
-    def h_copy(t):
-        return remote(tile.at[t], tile_box, h_send.at[0], h_recv.at[0], {"h": 1 - h})
-
-    def n_copy(q):
-        peer = {"x": 2 * (1 - low) + h, "z": 2 * div(z, 2) + q // 2, "h": jnp.int32(q % 2)}
+    def n_copy(t, q):
+        peer = {"x": 2 * (1 - low) + t, "z": 2 * div(z, 2) + q // 2, "h": jnp.int32(q % 2)}
         slot = 2 * x + lax.rem(z, 2)
         own_slot = (peer["x"] == x) & (peer["z"] == z) & (peer["h"] == h)
         return slot, own_slot, remote(
-            tile.at[h, pl.ds(32 * q, 32)], in_n.at[slot], out_n_sem.at[q], in_n_sem.at[slot], peer
+            tile.at[t, pl.ds(32 * q, 32)], in_n.at[h, slot], out_n_sem.at[t, q], in_n_sem.at[h, slot], peer
         )
 
-    def t_copy(q):
+    def t_copy(t, q):
         peer = {
             "x": 2 * low + div(x, 2),
             "z": 4 * lax.rem(x, 2) + 2 * lax.rem(z, 2) + q // 2,
             "h": jnp.int32(q % 2),
             "l": 1 - low,
         }
-        slot = 4 * h + div(z, 2)
+        slot = 4 * t + div(z, 2)
         return remote(
-            tile_t.at[pl.ds(32 * q, 32)], in_t.at[slot], out_t_sem.at[q], in_t_sem.at[slot], peer
+            tile_t.at[t, pl.ds(32 * q, 32)], in_t.at[h, slot], out_t_sem.at[t, q], in_t_sem.at[h, slot], peer
         )
 
     def cross_z_done(t):
@@ -418,27 +414,18 @@
                     e_part[t, z, into, :] + e_box[t, 0, side, 0, rows, :] + e_box[t, 1, side, 0, rows, :]
                 )
 
-        @pl.when(h != t)
-        def _():
-            h_copy(t).start()
-
-        @pl.when(h == t)
-        def _():
-            h_copy(t).wait_recv()
-            total = tile[t] + tile_box[...]
-            tile[t] = total
-            tile_t[...] = total.T
-            for q in range(4):
-                t_copy(q).start()
-                slot, own_slot, copy = n_copy(q)
-
-                @pl.when(jnp.logical_not(own_slot))
-                def _():
-                    copy.start()
-
-                @pl.when(own_slot)
-                def _():
-                    in_n[slot] = tile[t, pl.ds(32 * q, 32), :]
+        tile_t[t] = tile[t].T
+        for q in range(4):
+            t_copy(t, q).start()
+            slot, own_slot, copy = n_copy(t, q)
+
+            @pl.when(jnp.logical_not(own_slot))
+            def _():
+                copy.start()
+
+            @pl.when(own_slot)
+            def _():
+                in_n[h, slot] = tile[t, pl.ds(32 * q, 32), :]
 
     def own_z_done():
         ring_d.arrived()
@@ -591,32 +578,34 @@
 
     @pl.when(div(x, 2) != low)
     def _():
-        here = x - 2 * (1 - low) == h
         for s in range(8):
-
-            @pl.when(jnp.logical_not(here & (2 * x + lax.rem(z, 2) == s)))
-            def _():
-                remote(in_n.at[s], in_n.at[s], out_n_sem.at[0], in_n_sem.at[s], {"h": 1 - h}).wait_recv()
-
-            remote(in_t.at[s], in_t.at[s], out_t_sem.at[0], in_t_sem.at[s], {"h": 1 - h}).wait_recv()
-            out_ref[:, s * 128 : (s + 1) * 128] = in_n[s] + in_t[s]
+            for g in range(2):
+
+                @pl.when(jnp.logical_not((h == g) & (2 * x + lax.rem(z, 2) == s)))
+                def _():
+                    box = in_n.at[g, s]
+                    remote(box, box, out_n_sem.at[0, 0], in_n_sem.at[g, s], {"h": 1 - h}).wait_recv()
+
+                box = in_t.at[g, s]
+                remote(box, box, out_t_sem.at[0, 0], in_t_sem.at[g, s], {"h": 1 - h}).wait_recv()
+            out_ref[:, s * 128 : (s + 1) * 128] = (in_n[0, s] + in_n[1, s]) + (in_t[0, s] + in_t[1, s])
 
     for j in range(len(CHUNKS)):
         y_copy(j).wait_send()
         s_copy(j, mine).wait_send()
     for ring in (ring_d, ring_f, *ring_c, *ring_e):
         ring.drain()
-    h_copy(1 - h).wait_send()
     for k in range(4):
         b_copy(k).wait_send()
     dh_copy().wait_send()
-    for q in range(4):
-        t_copy(q).wait_send()
-        _, own_slot, n_out = n_copy(q)
-
-        @pl.when(jnp.logical_not(own_slot))
-        def _():
-            n_out.wait_send()
+    for t in range(2):
+        for q in range(4):
+            t_copy(t, q).wait_send()
+            _, own_slot, n_out = n_copy(t, q)
+
+            @pl.when(jnp.logical_not(own_slot))
+            def _():
+                n_out.wait_send()
 
     stays, straight = straight_copy()
 
@@ -675,8 +664,7 @@
             f32(4, 32, 640),
             f32(2, 2, 2, 16, 640),
             f32(2, 128, 128),
-            f32(128, 128),
-            f32(128, 128),
+            f32(2, 128, 128),
             f32(32, 640),
             f32(32, 640),
             f32(32, 640),
@@ -684,8 +672,8 @@
             f32(3, 128, 128),
             f32(32, 640),
             f32(3, 4, 32, 128),
-            f32(8, 32, 128),
-            f32(8, 32, 128),
+            f32(2, 8, 32, 128),
+            f32(2, 8, 32, 128),
             dma((loads,)),
             dma((chunks,)),
             dma((chunks,)),
@@ -705,12 +693,12 @@
             dma((2,)),
             dma((1,)),
             dma((3, 4)),
-            dma((8,)),
-            dma((8,)),
+            dma((2, 8)),
+            dma((2, 8)),
             dma((1,)),
             dma((3, 2)),
-            dma((4,)),
-            dma((4,)),
+            dma((2, 4)),
+            dma((2, 4)),
         ],
         compiler_params=pltpu.CompilerParams(
             collective_id=0, has_side_effects=True, vmem_limit_bytes=60 * 1024 * 1024

time: 93.7 us -> 87.6 us (0.935)
  Pallas kernels: 91.2 us -> 85.1 us
    pallas_call x1, Pallas kernels: 91.2 us -> 85.1 us  [per_device(): pl.pallas_call(kernel, out_shape=jax.ShapeDtypeStruct((32, cols), jnp.flo...]
where the time goes in v5:
time: 87.6 us; the launch traced here: 87.4 us
  Pallas kernels  85.1 us (97%)
  local copies, waits for them, and re-layouts  1.69 us (2%)
    pallas_call x1, Pallas kernels, per_device(): pl.pallas_call(kernel, out_shape=jax.ShapeDtypeStruct((32, cols), jnp.flo...  85.1 us

profile of v5, /device:TPU:6, one launch (start us, length us, event | category | flops | bytes accessed | tf_op | source)
XLA Modules:
  0.0 87.4 jit_solution(1805930864607129286)
XLA Ops:
  0.7 85.1 %shard_map.37 = f32[32,1024]{1,0:T(8,128)} custom-call(f32[24,128]{1,0:T(8,128)} %bitcast.3, f32[1]{0:T(128)S(6)} %copy.5.w_ref, bf16[3072,1024]{1,0:T(8,128)(2,1)} %x_hbm.1), custom_call_target="tpu_custom_call" | custom-call | tf_op jit(solution)/shard_map/pallas_call | solution.py:637
  85.7 1.7 %copy.4 = f32[32,1,1024]{2,1,0:T(1,128)} copy(f32[32,1,1024]{2,0,1:T(8,128)} %bitcast.2) | data formatting | bytes 262144 | tf_op jit(solution)/shard_map/broadcast_in_dim | solution.py:707

commit v6 on v5

--- a/solution.py
+++ b/solution.py
@@ -542,13 +542,13 @@
     ring_e[1].begin_all()
     run(ring_e[0], 2)
     run(ring_e[1], 0)
-    own_h_done()
     run(ring_e[0], 3)
     run(ring_e[1], 1)
     run(ring_e[0], 4)
     run(ring_e[1], 2)
+    run(ring_e[1], 3)
+    own_h_done()
     cross_z_done(0)
-    run(ring_e[1], 3)
     run(ring_e[1], 4)
     cross_z_done(1)
 

time: 87.6 us -> 87.4 us (level); the launches traced: 87.4 us -> 86.2 us
  Pallas kernels: 85.1 us -> 83.8 us
    pallas_call x1, Pallas kernels: 85.1 us -> 83.8 us  [per_device(): pl.pallas_call(kernel, out_shape=jax.ShapeDtypeStruct((32, cols), jnp.flo...]
where the time goes in v6:
time: 87.4 us; the launch traced here: 86.2 us
  Pallas kernels  83.8 us (96%)
  local copies, waits for them, and re-layouts  1.69 us (2%)
    pallas_call x1, Pallas kernels, per_device(): pl.pallas_call(kernel, out_shape=jax.ShapeDtypeStruct((32, cols), jnp.flo...  83.8 us

profile of v6, /device:TPU:6, one launch (start us, length us, event | category | flops | bytes accessed | tf_op | source)
XLA Modules:
  0.0 86.2 jit_solution(2684123113586608149)
XLA Ops:
  0.7 83.8 %shard_map.37 = f32[32,1024]{1,0:T(8,128)} custom-call(f32[24,128]{1,0:T(8,128)} %bitcast.3, f32[1]{0:T(128)S(6)} %copy.5.w_ref, bf16[3072,1024]{1,0:T(8,128)(2,1)} %x_hbm.1), custom_call_target="tpu_custom_call" | custom-call | tf_op jit(solution)/shard_map/pallas_call | solution.py:637
  84.5 1.7 %copy.4 = f32[32,1,1024]{2,1,0:T(1,128)} copy(f32[32,1,1024]{2,0,1:T(8,128)} %bitcast.2) | data formatting | bytes 262144 | tf_op jit(solution)/shard_map/broadcast_in_dim | solution.py:707
